TPU v7x, 512 devices: a whole 4x4x16 slice. The times are simulated.
512 devices in a mesh: dp: 4 (over y), row: 16 (over x, z_lo), col: 8 (over z_hi, core).
Axes of the slice: x: 4, y: 4, z: 16 (z_hi: 4, z_lo: 4; z = z_hi * 4 + z_lo), core: 2. Of those that a mesh axis runs over, the one named last changes fastest.
Arguments:
- grad_parts: float32 [4, 4, 1024, 10240], P('dp', None, 'row', 'col'), may hold values from -120 to 120, as said below
- gauss_noise: float32 [4096, 10240], P(('dp', 'row'), 'col'), may hold values from -6 to 6
- blt_buffers: float32 [4, 4096, 10240], P(None, ('dp', 'row'), 'col'), may hold values from -4 to 4
- blt_decays: float32 [4], replicated, may hold values from 0.2 to 0.98
- blt_weights: float32 [4], replicated, may hold values from 0.1 to 0.6
- master_weights: float32 [4096, 10240], P(('dp', 'row'), 'col'), may hold values from -4 to 4
- row_stat: float32 [4096], P(('dp', 'row')), may hold values from 0.05 to 0.5
- col_stat: float32 [10240], P('col'), may hold values from 0.05 to 0.5
Outputs:
- direction: float32 [4096, 10240], P(('dp', 'row'), 'col')
- weight_copy: bfloat16 [4096, 10240], P(('dp', 'row'), 'col')
- new_buffers: float32 [4, 4096, 10240], P(None, ('dp', 'row'), 'col')
- new_row_stat: float32 [4096], P(('dp', 'row'))
- new_col_stat: float32 [10240], P('col')
Inputs may be any that keep to these rules, and one draw needn't show every extreme that they name: `grad_parts`: finite real values.
All inputs are finite; a program needn't handle non-finite values.
Results may differ from a plain program's by a relative error of at most 0.001.
Values sent between devices are 32-bit elements; how exact they have to be, the bound alone decides.
No kernel may reach another device: no remote copies, remote signals or barrier semaphores. Data moves between devices by JAX's collectives and lax.ppermute only.
A program may use at most 64 MiB of HBM per device.

v0:
```python
import jax
import jax.numpy as jnp
from jax import lax
from jax.sharding import Mesh
from jax.sharding import PartitionSpec as P

D = 4096
FF = 10240
NOISE_STD = 2.0
DECAY_RATE = 0.85
LEARN_RATE = 0.01
TINY_TERM = 1e-30
ROW = ("x", "zl")
COL = ("zh", "core")
RUN = ("zl", "core")
PLANE = ("dp", "x")


def sum_of_sent(messages, axes):
    arrived = lax.all_to_all(messages, axes, split_axis=0, concat_axis=0, tiled=True)
    return arrived.sum(axis=0)


def per_device(
    grad_parts,
    gauss_noise,
    blt_buffers,
    blt_decays,
    blt_weights,
    master_weights,
    row_stat,
    col_stat,
):
    rows, cols = gauss_noise.shape
    n_col, n_run, n_plane = (lax.axis_size(axes) for axes in (COL, RUN, PLANE))
    arrived = lax.all_to_all(
        grad_parts.reshape(-1, rows, cols), "dp", split_axis=0, concat_axis=0, tiled=True
    )
    correlated = gauss_noise - jnp.sum(blt_buffers * blt_weights[:, None, None], axis=0)
    new_buffers = blt_decays[:, None, None] * blt_buffers + correlated[None]
    to = jnp.arange(n_run)
    same_cols = (to % 2 == lax.axis_index("core")).astype(jnp.float32)
    same_rows = (to // 2 == lax.axis_index("zl")).astype(jnp.float32)
    takes = jnp.concatenate(
        [
            jnp.broadcast_to(same_cols[:, None], (n_run, cols)),
            jnp.ones((n_run, rows), jnp.float32),
            jnp.broadcast_to(same_rows[:, None], (n_run, rows)),
        ],
        axis=1,
    )
    ones = jnp.broadcast_to(same_cols[0] + same_cols[1], (rows, rows))
    arrived, correlated, new_buffers, takes, row_stat, ones = lax.optimization_barrier(
        (arrived, correlated, new_buffers, takes, row_stat, ones)
    )
    noisy = arrived.sum(axis=0) + NOISE_STD * correlated
    squares = noisy * noisy
    share = DECAY_RATE / n_col * row_stat + (1.0 - DECAY_RATE) * (
        jnp.sum(squares, axis=1) / FF + TINY_TERM / n_col
    )
    sums = jnp.concatenate([jnp.sum(squares, axis=0), share, share])
    sums, col_stat, master_weights, takes = lax.optimization_barrier(
        (sums, col_stat, master_weights, takes)
    )
    run = sum_of_sent(sums[None] * takes, RUN)
    run, own = lax.optimization_barrier((run, run[cols + rows :]))
    plane = sum_of_sent(jnp.broadcast_to(run[None], (n_plane, *run.shape)), PLANE)
    stats = jnp.concatenate([plane[cols : cols + rows], own])
    new_col = DECAY_RATE * col_stat + (1.0 - DECAY_RATE) * (plane[:cols] / D + TINY_TERM)
    stats, new_col = lax.optimization_barrier((stats, new_col))
    stats = lax.psum(stats, "zh")
    shares, new_row = lax.optimization_barrier((stats[:rows], stats[rows:]))
    row_mean = jnp.sum(ones * shares[None, :], axis=1) / D
    direction = noisy / jnp.sqrt((new_row / row_mean)[:, None] * new_col[None, :])
    weight_copy = (master_weights - LEARN_RATE * direction).astype(jnp.bfloat16)
    return (direction, weight_copy, new_buffers, new_row, new_col)


def solution(mesh):
    finer = Mesh(
        mesh.devices.reshape(mesh.shape["dp"], 4, 4, 4, 2), ("dp", "x", "zl", "zh", "core")
    )
    rows = ("dp", *ROW)
    return jax.shard_map(
        per_device,
        mesh=finer,
        in_specs=(
            P("dp", None, ROW, COL),
            P(rows, COL),
            P(None, rows, COL),
            P(),
            P(),
            P(rows, COL),
            P(rows),
            P(COL),
        ),
        out_specs=(P(rows, COL), P(rows, COL), P(None, rows, COL), P(rows), P(COL)),
        check_vma=False,
    )
```

profile of v0, /device:TPU:2, one launch (start us, length us, event | category | flops | bytes accessed | tf_op | source)
XLA Modules:
  0.0 66.8 jit_solution(16642398468333567956)
XLA Ops:
  0.6 0.0 copy-start
  0.6 0.0 copy-start.5
  0.7 4.6 %all-to-all-start = ((f32[4,64,1280]{2,1,0:T(8,128)}), f32[4,64,1280]{2,1,0:T(8,128)S(1)}, u32[]{:S(2)}, u32[]{:S(2)}) async-start(f32[4,64,1280]{2,1,0:T(8,128)} %bitcast.2), calls=%async_computation | async-start | bytes 2621440 | tf_op jit(solution)/shard_map/all_to_all | solution.py:36
  5.3 0.0 copy-start.1
  5.3 0.6 fusion.4
  7.2 0.0 copy-done
  7.2 0.0 copy-done.5
  7.2 0.0 copy-start.6
  7.2 0.2 multiply_reduce_fusion
  7.3 0.0 copy-done.1
  7.4 0.1 broadcast_in_dim.12
  7.5 0.1 broadcast_in_dim.10
  7.6 0.1 concatenate.9
  7.6 0.2 copy-done.6
  7.8 1.2 %multiply_add_fusion = f32[4,64,1280]{2,1,0:T(8,128)} fusion(f32[4,64,1280]{2,1,0:T(8,128)S(1)} %copy-done, f32[64,1280]{1,0:T(8,128)S(1)} %sub.10, f32[4]{0:T(128)S(1)} %copy-done.6), kind=kLoop, calls=%fused_computation | loop fusion | flops 655360 | bytes 2949136 | tf_op jit(solution)/shard_map/add | solution.py:40
  9.1 0.0 copy-start.8
  9.1 14.1 %all-to-all-done = f32[4,64,1280]{2,1,0:T(8,128)S(1)} async-done(((f32[4,64,1280]{2,1,0:T(8,128)}), f32[4,64,1280]{2,1,0:T(8,128)S(1)}, u32[]{:S(2)}, u32[]{:S(2)}) %all-to-all-start) | async-done | bytes 1310752 | tf_op jit(solution)/shard_map/all_to_all | solution.py:36
  23.2 0.0 copy-start.4
  23.2 0.0 copy-start.2
  23.2 0.1 reduce_sum.64
  23.3 0.2 multiply_reduce_fusion.1
  23.4 0.0 copy-done.8
  23.4 0.1 concatenate.10
  23.6 11.5 %all_to_all.20 = f32[8,1,1408]{2,1,0:T(1,128)S(1)} all-to-all(f32[8,1,1408]{2,1,0:T(1,128)S(1)} %all_to_all.14), channel_id=1, replica_groups=mesh['dp'=4,'x'=4,'zl'=4,'zh'=4,'core'=2] {'zl','core'}, dimensions={0} | all-to-all | bytes 90112 | tf_op jit(solution)/shard_map/all_to_all | solution.py:20
  35.1 0.1 slice.28
  35.2 11.7 %all_to_all.21 = f32[16,1,1408]{2,1,0:T(1,128)S(1)} all-to-all(f32[16,1,1408]{2,1,0:T(1,128)S(1)} %broadcast_in_dim.14), channel_id=1, replica_groups=mesh['dp'=4,'x'=4,'zl'=4,'zh'=4,'core'=2] {'dp','x'}, dimensions={0} | all-to-all | bytes 180224 | tf_op jit(solution)/shard_map/all_to_all | solution.py:20
  46.9 0.1 reduce_sum.68
  47.0 0.0 copy-done.4
  47.0 0.0 copy-start.3
  47.0 0.1 pad_maximum_fusion
  47.1 18.5 %psum.7 = f32[128]{0:T(128)S(1)} all-reduce(f32[128]{0:T(128)S(1)} %pad_maximum_fusion), channel_id=1, replica_groups=mesh['dp'=4,'x'=4,'zl'=4,'zh'=4,'core'=2] {'zh'}, use_global_device_ids=true, to_apply=%region_6.7 | all-reduce | flops 128 | bytes 1024 | tf_op jit(solution)/shard_map/psum | solution.py:71
  65.6 0.1 fusion.3
  65.7 0.0 copy-start.7
  65.7 0.1 multiply_reduce_fusion.3
  65.8 0.0 copy-done.2
  65.8 0.9 %subtract_convert_fusion = (bf16[64,1280]{1,0:T(8,128)(2,1)}, f32[64,1280]{1,0:T(8,128)}) fusion(f32[64,1280]{1,0:T(8,128)S(1)} %copy-done.2, f32[1280]{0:T(1024)S(1)} %fusion.2, f32[64]{0:T(128)S(1)} %multiply_divide_fusion, f32[64,1280]{1,0:T(8,128)S(1)} %reduce_sum.64, f32[64,1280]{1,0:T(8,128)S(1)} %sub.10), kind=kLoop, calls=%fused_computation.2 | loop fusion | flops 573440 | bytes 1479936 | tf_op jit(solution)/shard_map/convert_element_type | solution.py:75
  66.8 0.0 copy-done.3
  66.8 0.0 copy-done.7
  (13 shorter events, 0.2 us)
Async XLA Ops:
  0.6 6.5 %copy-start = (f32[4,64,1280]{2,1,0:T(8,128)S(1)}, f32[4,64,1280]{2,1,0:T(8,128)}, u32[]{:S(2)}) copy-start(f32[4,64,1280]{2,1,0:T(8,128)} %param.10) | copy-start | bytes 3932164
  0.6 6.5 %copy-start.5 = (f32[4]{0:T(128)S(1)}, f32[4]{0:T(128)}, u32[]{:S(2)}) copy-start(f32[4]{0:T(128)} %param.12) | copy-start | bytes 52
  0.7 22.5 %all-to-all-start = ((f32[4,64,1280]{2,1,0:T(8,128)}), f32[4,64,1280]{2,1,0:T(8,128)S(1)}, u32[]{:S(2)}, u32[]{:S(2)}) async-start(f32[4,64,1280]{2,1,0:T(8,128)} %bitcast.2), calls=%async_computation | async-start | bytes 2621440 | tf_op jit(solution)/shard_map/all_to_all | solution.py:36
  5.3 2.1 %copy-start.1 = (f32[64,1280]{1,0:T(8,128)S(1)}, f32[64,1280]{1,0:T(8,128)}, u32[]{:S(2)}) copy-start(f32[64,1280]{1,0:T(8,128)} %param.9) | copy-start | bytes 983044
  7.2 0.7 copy-start.6
  9.1 14.4 %copy-start.8 = (f32[64]{0:T(128)S(1)}, f32[64]{0:T(128)}, u32[]{:S(2)}) copy-start(f32[64]{0:T(128)} %param.14) | copy-start | bytes 772
  23.2 23.8 %copy-start.4 = (f32[1280]{0:T(1024)S(1)}, f32[1280]{0:T(1024)}, u32[]{:S(2)}) copy-start(f32[1280]{0:T(1024)} %param.15) | copy-start | bytes 15364
  23.2 42.7 %copy-start.2 = (f32[64,1280]{1,0:T(8,128)S(1)}, f32[64,1280]{1,0:T(8,128)}, u32[]{:S(2)}) copy-start(f32[64,1280]{1,0:T(8,128)} %param.13) | copy-start | bytes 983044
  47.0 19.8 %copy-start.3 = (f32[1280]{0:T(1024)}, f32[1280]{0:T(1024)S(1)}, u32[]{:S(2)}) copy-start(f32[1280]{0:T(1024)S(1)} %fusion.2) | copy-start | bytes 15364
  65.7 1.1 %copy-start.7 = (f32[64]{0:T(128)}, f32[64]{0:T(128)S(1)}, u32[]{:S(2)}) copy-start(f32[64]{0:T(128)S(1)} %get-tuple-element.19) | copy-start | bytes 772
where the time goes:
time: 67.1 us; the launch traced here: 66.8 us
  blocking collectives  41.7 us (62%)
  waiting for transfers between devices  14.1 us (21%)
  starting transfers between devices  4.61 us (7%)
  other arithmetic  2.93 us (4%)
  between operations  2.1 us (3%)
  local copies, waits for them, and re-layouts  1.35 us (2%)
    all_to_all x2, blocking collectives, sum_of_sent(): lax.all_to_all(messages, axes, split_axis=0, concat_axis=0, tiled=True)  23.2 us
    psum x1, blocking collectives, per_device(): stats = lax.psum(stats, 'zh')  18.5 us
    all_to_all x1, waiting for transfers between devices, per_device(): lax.all_to_all(grad_parts.reshape(-1, rows, cols), 'dp', split_axis=0, co...  14.1 us
    all_to_all x1, starting transfers between devices, per_device(): lax.all_to_all(grad_parts.reshape(-1, rows, cols), 'dp', split_axis=0, co...  4.61 us
  transfers between devices with their start and end apart: 1, of which 1 were waited for; matrix products, arithmetic and copies ran while one was open for 3% of the time, Pallas kernels for 0%

commit v1 on v0

--- a/solution.py
+++ b/solution.py
@@ -68,7 +68,7 @@
     stats = jnp.concatenate([plane[cols : cols + rows], own])
     new_col = DECAY_RATE * col_stat + (1.0 - DECAY_RATE) * (plane[:cols] / D + TINY_TERM)
     stats, new_col = lax.optimization_barrier((stats, new_col))
-    stats = lax.psum(stats, "zh")
+    stats = jnp.sum(lax.all_gather(stats, "zh"), axis=0)
     shares, new_row = lax.optimization_barrier((stats[:rows], stats[rows:]))
     row_mean = jnp.sum(ones * shares[None, :], axis=1) / D
     direction = noisy / jnp.sqrt((new_row / row_mean)[:, None] * new_col[None, :])

time: 67.1 us -> 66.3 us (0.988)
  blocking collectives: 41.7 us -> 40.9 us
    psum x1 -> x0, blocking collectives: 18.5 us -> none  [per_device(): stats = lax.psum(stats, 'zh')]
    all_gather x0 -> x1, blocking collectives: none -> 17.8 us  [per_device(): stats = jnp.sum(lax.all_gather(stats, 'zh'), axis=0)]
where the time goes in v1:
time: 66.3 us; the launch traced here: 66 us
  blocking collectives  40.9 us (62%)
  waiting for transfers between devices  14.1 us (21%)
  starting transfers between devices  4.61 us (7%)
  other arithmetic  2.95 us (4%)
  between operations  2.1 us (3%)
  local copies, waits for them, and re-layouts  1.35 us (2%)
    all_to_all x2, blocking collectives, sum_of_sent(): lax.all_to_all(messages, axes, split_axis=0, concat_axis=0, tiled=True)  23.2 us
    all_gather x1, blocking collectives, per_device(): stats = jnp.sum(lax.all_gather(stats, 'zh'), axis=0)  17.8 us
    all_to_all x1, waiting for transfers between devices, per_device(): lax.all_to_all(grad_parts.reshape(-1, rows, cols), 'dp', split_axis=0, co...  14.1 us
    all_to_all x1, starting transfers between devices, per_device(): lax.all_to_all(grad_parts.reshape(-1, rows, cols), 'dp', split_axis=0, co...  4.61 us
  transfers between devices with their start and end apart: 1, of which 1 were waited for; matrix products, arithmetic and copies ran while one was open for 3% of the time, Pallas kernels for 0%

profile of v1, /device:TPU:2, one launch (start us, length us, event | category | flops | bytes accessed | tf_op | source)
XLA Modules:
  0.0 66.0 jit_solution(1717628756001904822)
XLA Ops:
  0.6 0.0 copy-start
  0.6 0.0 copy-start.5
  0.7 4.6 %all-to-all-start = ((f32[4,64,1280]{2,1,0:T(8,128)}), f32[4,64,1280]{2,1,0:T(8,128)S(1)}, u32[]{:S(2)}, u32[]{:S(2)}) async-start(f32[4,64,1280]{2,1,0:T(8,128)} %bitcast.3), calls=%async_computation | async-start | bytes 2621440 | tf_op jit(solution)/shard_map/all_to_all | solution.py:36
  5.3 0.0 copy-start.1
  5.3 0.6 fusion.4
  7.2 0.0 copy-done
  7.2 0.0 copy-done.5
  7.2 0.0 copy-start.6
  7.2 0.2 multiply_reduce_fusion
  7.3 0.0 copy-done.1
  7.4 0.1 broadcast_in_dim.12
  7.5 0.1 broadcast_in_dim.10
  7.6 0.1 concatenate.9
  7.6 0.2 copy-done.6
  7.8 1.2 %multiply_add_fusion = f32[4,64,1280]{2,1,0:T(8,128)} fusion(f32[4,64,1280]{2,1,0:T(8,128)S(1)} %copy-done, f32[64,1280]{1,0:T(8,128)S(1)} %sub.10, f32[4]{0:T(128)S(1)} %copy-done.6), kind=kLoop, calls=%fused_computation | loop fusion | flops 655360 | bytes 2949136 | tf_op jit(solution)/shard_map/add | solution.py:40
  9.1 0.0 copy-start.8
  9.1 14.1 %all-to-all-done = f32[4,64,1280]{2,1,0:T(8,128)S(1)} async-done(((f32[4,64,1280]{2,1,0:T(8,128)}), f32[4,64,1280]{2,1,0:T(8,128)S(1)}, u32[]{:S(2)}, u32[]{:S(2)}) %all-to-all-start) | async-done | bytes 1310752 | tf_op jit(solution)/shard_map/all_to_all | solution.py:36
  23.2 0.0 copy-start.4
  23.2 0.0 copy-start.2
  23.2 0.1 reduce_sum.73
  23.3 0.2 multiply_reduce_fusion.1
  23.4 0.0 copy-done.8
  23.4 0.1 concatenate.10
  23.6 11.5 %all_to_all.20 = f32[8,1,1408]{2,1,0:T(1,128)S(1)} all-to-all(f32[8,1,1408]{2,1,0:T(1,128)S(1)} %all_to_all.14), channel_id=1, replica_groups=mesh['dp'=4,'x'=4,'zl'=4,'zh'=4,'core'=2] {'zl','core'}, dimensions={0} | all-to-all | bytes 90112 | tf_op jit(solution)/shard_map/all_to_all | solution.py:20
  35.1 0.1 slice.28
  35.2 11.7 %all_to_all.21 = f32[16,1,1408]{2,1,0:T(1,128)S(1)} all-to-all(f32[16,1,1408]{2,1,0:T(1,128)S(1)} %broadcast_in_dim.14), channel_id=1, replica_groups=mesh['dp'=4,'x'=4,'zl'=4,'zh'=4,'core'=2] {'dp','x'}, dimensions={0} | all-to-all | bytes 180224 | tf_op jit(solution)/shard_map/all_to_all | solution.py:20
  46.9 0.1 reduce_sum.77
  47.0 0.0 copy-done.4
  47.0 0.0 copy-start.3
  47.0 0.1 pad_maximum_fusion
  47.1 17.8 %all-gather.1 = f32[4,1,128]{2,1,0:T(1,128)S(1)} all-gather(f32[1,1,128]{2,1,0:T(1,128)S(1)} %bitcast.4), channel_id=2, replica_groups=mesh['dp'=4,'x'=4,'zl'=4,'zh'=4,'core'=2] {'zh'}, dimensions={0}, use_global_device_ids=true | all-gather | bytes 2560 | tf_op jit(solution)/shard_map/all_gather | solution.py:71
  64.9 0.1 fusion.3
  65.0 0.0 copy-start.7
  65.0 0.1 multiply_reduce_fusion.3
  65.1 0.0 copy-done.2
  65.1 0.9 %subtract_convert_fusion = (bf16[64,1280]{1,0:T(8,128)(2,1)}, f32[64,1280]{1,0:T(8,128)}) fusion(f32[64,1280]{1,0:T(8,128)S(1)} %copy-done.2, f32[1280]{0:T(1024)S(1)} %fusion.2, f32[64]{0:T(128)S(1)} %multiply_divide_fusion, f32[64,1280]{1,0:T(8,128)S(1)} %reduce_sum.73, f32[64,1280]{1,0:T(8,128)S(1)} %sub.10), kind=kLoop, calls=%fused_computation.2 | loop fusion | flops 573440 | bytes 1479936 | tf_op jit(solution)/shard_map/convert_element_type | solution.py:75
  66.0 0.0 copy-done.3
  66.0 0.0 copy-done.7
  (14 shorter events, 0.2 us)
Async XLA Ops:
  0.6 6.5 %copy-start = (f32[4,64,1280]{2,1,0:T(8,128)S(1)}, f32[4,64,1280]{2,1,0:T(8,128)}, u32[]{:S(2)}) copy-start(f32[4,64,1280]{2,1,0:T(8,128)} %param.10) | copy-start | bytes 3932164
  0.6 6.5 %copy-start.5 = (f32[4]{0:T(128)S(1)}, f32[4]{0:T(128)}, u32[]{:S(2)}) copy-start(f32[4]{0:T(128)} %param.12) | copy-start | bytes 52
  0.7 22.5 %all-to-all-start = ((f32[4,64,1280]{2,1,0:T(8,128)}), f32[4,64,1280]{2,1,0:T(8,128)S(1)}, u32[]{:S(2)}, u32[]{:S(2)}) async-start(f32[4,64,1280]{2,1,0:T(8,128)} %bitcast.3), calls=%async_computation | async-start | bytes 2621440 | tf_op jit(solution)/shard_map/all_to_all | solution.py:36
  5.3 2.1 %copy-start.1 = (f32[64,1280]{1,0:T(8,128)S(1)}, f32[64,1280]{1,0:T(8,128)}, u32[]{:S(2)}) copy-start(f32[64,1280]{1,0:T(8,128)} %param.9) | copy-start | bytes 983044
  7.2 0.7 copy-start.6
  9.1 14.4 %copy-start.8 = (f32[64]{0:T(128)S(1)}, f32[64]{0:T(128)}, u32[]{:S(2)}) copy-start(f32[64]{0:T(128)} %param.14) | copy-start | bytes 772
  23.2 23.8 %copy-start.4 = (f32[1280]{0:T(1024)S(1)}, f32[1280]{0:T(1024)}, u32[]{:S(2)}) copy-start(f32[1280]{0:T(1024)} %param.15) | copy-start | bytes 15364
  23.2 41.9 %copy-start.2 = (f32[64,1280]{1,0:T(8,128)S(1)}, f32[64,1280]{1,0:T(8,128)}, u32[]{:S(2)}) copy-start(f32[64,1280]{1,0:T(8,128)} %param.13) | copy-start | bytes 983044
  47.0 19.0 %copy-start.3 = (f32[1280]{0:T(1024)}, f32[1280]{0:T(1024)S(1)}, u32[]{:S(2)}) copy-start(f32[1280]{0:T(1024)S(1)} %fusion.2) | copy-start | bytes 15364
  65.0 1.1 %copy-start.7 = (f32[64]{0:T(128)}, f32[64]{0:T(128)S(1)}, u32[]{:S(2)}) copy-start(f32[64]{0:T(128)S(1)} %get-tuple-element.19) | copy-start | bytes 772
